TPU v7x, 256 devices: a whole 4x4x8 slice. The times are simulated.
256 devices in a mesh: gx: 64 (over z_lo, x, y), gy: 4 (over z_hi, core).
Axes of the slice: x: 4, y: 4, z: 8 (z_hi: 2, z_lo: 4; z = z_hi * 4 + z_lo), core: 2. Of those that a mesh axis runs over, the one named last changes fastest.
Arguments:
- date_key: int32 [3145728], P(('gx', 'gy')), may hold values from 0 to 4095
- store_key: int32 [3145728], P(('gx', 'gy')), may hold values from 0 to 65535
- product_key: int32 [3145728], P(('gx', 'gy')), may hold values from 0 to 1048575
- revenue: bfloat16 [3145728], P(('gx', 'gy')), may hold values from -0.59765625 to 0.59765625
- row_counts: int32 [256], P(('gx', 'gy')), may hold values from 1 to 12288, 1966080 in all
- date_years: int32 [512], P('gx'), may hold values from -2147483648 to 2147483646
- date_flags: int32 [128], P('gx'), may hold values from -2147483648 to 2147483646
- store_flags: int32 [2048], P('gx'), may hold values from -2147483648 to 2147483646
- product_flags: int32 [32768], P('gx'), may hold values from -2147483648 to 2147483646
- brand_words: int32 [349696], P('gx'), may hold values from 0 to 1073741823
Outputs:
- revenue_groups: float32 [16, 1024], replicated
Inputs may be any that keep to these rules, and one draw needn't show every extreme that they name: Rows d * 12288 to d * 12288 + row_counts[d] - 1 of the fact arrays are live; the largest count equals 12288. `date_years`: date k's year code is in bits 4 * (k % 8) of word k // 8. `date_flags`: bit k % 32 of word k // 32 is the flag of row k. `store_flags`: bit k % 32 of word k // 32 is the flag of row k. `product_flags`: bit k % 32 of word k // 32 is the flag of row k. `brand_words`: product with shard o and local index l holds its brand code in bits 10 * (l % 3) of word o * 5464 + l // 3; words past a shard's products are unused.
All inputs are finite; a program needn't handle non-finite values. No bound on the sum of `row_counts` on one device may be relied on, other than what follows from the above.
Results may differ from a plain program's by a relative error of at most 0.0003.
Values sent between devices are 32-bit elements; how exact they have to be, the bound alone decides.
No kernel may reach another device: no remote copies, remote signals or barrier semaphores. Data moves between devices by JAX's collectives and lax.ppermute only.
A program may use at most 64 MiB of HBM per device.

v0:
```python
import jax
import jax.numpy as jnp
from jax import lax
from jax.sharding import PartitionSpec as P

BRANDS = 1024
YEARS = 16


def joined_along(blocks, dim):
    dims = list(blocks.shape[1:])
    dims[dim] *= blocks.shape[0]
    return jnp.moveaxis(blocks, 0, dim).reshape(dims)


def gather_together(arrays, axis, dims):
    flat = jnp.concatenate([a.reshape(-1) for a in arrays])
    lines, at, outs = (lax.all_gather(flat, axis), 0, [])
    for a, dim in zip(arrays, dims):
        blocks = lines[:, at : at + a.size].reshape(-1, *a.shape)
        outs.append(joined_along(blocks, dim))
        at += a.size
    return tuple(outs)


def from_everyone(value, axis):
    copies = jnp.broadcast_to(value, (lax.axis_size(axis), *value.shape))
    return lax.all_to_all(copies, axis, split_axis=0, concat_axis=0, tiled=True)


def collect(value, axis, dim):
    blocks = from_everyone(value, axis)
    return joined_along(blocks, dim)


def pick_bits(packed, position, width_bits):
    per_word = 32 // width_bits
    chosen = packed[position // per_word]
    shifted = jnp.right_shift(chosen, position % per_word * width_bits)
    return jnp.bitwise_and(shifted, (1 << width_bits) - 1)


def shards(
    date_key,
    store_key,
    product_key,
    revenue,
    row_counts,
    date_years,
    date_flags,
    store_flags,
    product_flags,
    brand_words,
):
    gx_count = lax.axis_size("gx")
    gy_count = lax.axis_size("gy")
    flag_shard = product_flags.shape[0]
    brand_shard = brand_words.shape[0]
    prod_shard = flag_shard * 32
    member = lax.axis_index("gy")
    brand_part = brand_shard // gy_count
    flag_part = flag_shard // gy_count
    brand_slice = lax.dynamic_slice_in_dim(brand_words, member * brand_part, brand_part, 0)
    flag_slice = lax.dynamic_slice_in_dim(product_flags, member * flag_part, flag_part, 0)
    year_words, date_bits, store_bits, flag_some, brand_some = gather_together(
        (date_years, date_flags, store_flags, flag_slice, brand_slice), "gx", (0, 0, 0, 0, 0)
    )
    product_bits, brand_table = (collect(flag_some, "gy", 0), collect(brand_some, "gy", 0))

    def brand_place(owner_idx, word_idx):
        return (
            word_idx // brand_part * (gx_count * brand_part)
            + owner_idx * brand_part
            + word_idx % brand_part
        )

    def flag_place(owner_idx, word_idx):
        return (
            word_idx // flag_part * (gx_count * flag_part)
            + owner_idx * flag_part
            + word_idx % flag_part
        )

    block_rows = min(4096, date_key.shape[0])
    row_count = row_counts[0]
    block_total = (row_count + block_rows - 1) // block_rows
    high_groups = YEARS * BRANDS // 128

    def add_block(block_idx, totals):
        first_row = block_idx * block_rows
        date_block = lax.dynamic_slice_in_dim(date_key, first_row, block_rows, 0)
        store_block = lax.dynamic_slice_in_dim(store_key, first_row, block_rows, 0)
        product_block = lax.dynamic_slice_in_dim(product_key, first_row, block_rows, 0)
        money_block = lax.dynamic_slice_in_dim(revenue, first_row, block_rows, 0)
        live_rows = first_row + lax.iota(jnp.int32, block_rows) < row_count
        year_code = pick_bits(year_words, date_block, 4)
        owner_idx = product_block // prod_shard
        local_idx = product_block % prod_shard
        flag_word = product_bits[flag_place(owner_idx, local_idx // 32)]
        product_pass = jnp.bitwise_and(jnp.right_shift(flag_word, local_idx % 32), 1)
        passed = (
            pick_bits(date_bits, date_block, 1)
            * pick_bits(store_bits, store_block, 1)
            * product_pass
        )
        word_val = brand_table[brand_place(owner_idx, local_idx // 3)]
        brand_code = jnp.bitwise_and(jnp.right_shift(word_val, local_idx % 3 * 10), 1023)
        kept_rows = live_rows & (passed == 1)
        amount = jnp.where(kept_rows, money_block, jnp.zeros_like(money_block))
        high_row = year_code * (BRANDS // 128) + brand_code // 128
        weighted = jnp.where(
            lax.iota(jnp.int32, high_groups)[:, None] == high_row[None, :],
            amount[None, :],
            jnp.zeros((), jnp.bfloat16),
        )
        low_hot = (lax.iota(jnp.int32, 128)[:, None] == (brand_code % 128)[None, :]).astype(
            jnp.bfloat16
        )
        return totals + lax.dot_general(
            weighted, low_hot, (((1,), (1,)), ((), ())), preferred_element_type=jnp.float32
        )

    totals = lax.fori_loop(0, block_total, add_block, jnp.zeros((high_groups, 128), jnp.float32))
    group_sums = totals.reshape(YEARS, BRANDS)
    result = lax.psum(group_sums, ("gx", "gy"))
    return result


def solution(mesh):
    placed = (
        P(("gx", "gy")),
        P(("gx", "gy")),
        P(("gx", "gy")),
        P(("gx", "gy")),
        P(("gx", "gy")),
        P("gx"),
        P("gx"),
        P("gx"),
        P("gx"),
        P("gx"),
    )
    return jax.shard_map(shards, mesh=mesh, in_specs=placed, out_specs=P(), check_vma=False)
```

profile of v0, /device:TPU:1, one launch (start us, length us, event | category | flops | bytes accessed | tf_op | source)
XLA Modules:
  0.0 855.9 jit_solution(2321840146524522188)
XLA Ops:
  6.5 0.8 dynamic_slice.34
  7.3 0.8 dynamic_slice.35
  8.1 0.8 concatenate.3
  8.8 163.3 %all-gather.1 = s32[64,1,1536]{2,1,0:T(1,128)S(1)} all-gather(s32[1,1,1536]{2,1,0:T(1,128)S(1)} %reshape.91), channel_id=2, replica_groups=mesh['gx'=64,'gy'=4] {'gx'}, dimensions={0}, use_global_device_ids=true | all-gather | bytes 399360 | tf_op jit(solution)/shard_map/all_gather | solution.py:18
  172.2 0.1 slice.31
  172.4 0.3 broadcast_in_dim.74
  172.7 1.8 broadcast_in_dim.75
  174.5 36.1 %all-to-all-start = ((s32[4,1,87424]{2,1,0:T(1,128)}), s32[4,1,87424]{2,1,0:T(1,128)S(1)}, u32[]{:S(2)}, u32[]{:S(2)}) async-start(s32[4,1,87424]{2,1,0:T(1,128)} %broadcast_in_dim.75), calls=%async_computation | async-start | bytes 2797568 | tf_op jit(solution)/shard_map/all_to_all | solution.py:28
  210.5 0.1 slice_bitcast_fusion
  210.6 21.0 %all-to-all-done = s32[4,1,87424]{2,1,0:T(1,128)S(1)} async-done(((s32[4,1,87424]{2,1,0:T(1,128)}), s32[4,1,87424]{2,1,0:T(1,128)S(1)}, u32[]{:S(2)}, u32[]{:S(2)}) %all-to-all-start) | async-done | bytes 1398816 | tf_op jit(solution)/shard_map/all_to_all | solution.py:28
  231.7 0.7 broadcast_in_dim.77
  232.4 4.3 all-to-all-start.1
  237.3 0.1 slice.33
  237.4 0.1 slice.32
  237.5 0.1 reshape.42
  237.6 0.1 reshape.41
  237.7 0.1 reshape.39
  237.8 4.3 reduce
  242.1 0.6 reshape.40
  242.7 1.4 all-to-all-done.1
  244.2 122.1 %while.13 = (s32[]{:T(128)}, f32[128,128]{1,0:T(8,128)S(1)}, s32[]{:T(128)}, s32[12288]{0:T(1024)S(1)}, s32[512]{0:T(512)S(1)}, /*index=5*/s32[12288]{0:T(1024)S...) while((s32[]{:T(128)}, f32[128,128]{1,0:T(8,128)S(1)}, ...), condition=%wide.region_1.2_spmd, body=%wide.region_0.1_spmd.sunk | while | flops 136892416 | bytes 860395 | solution.py:123
  244.2 23.0 %gather_fusion.2 = s32[4096]{0:T(1024)S(1)} fusion(s32[32768]{0:T(1024)S(1)} %get-tuple-element.431, s32[4096]{0:T(1024)S(1)} %get-tuple-element.382), kind=kCustom, calls=%fused_computation.4.clone.1 | custom fusion | bytes 49152 | tf_op jit(solution)/shard_map/while/body/gather | solution.py:99
  267.4 23.0 %gather_fusion.1 = s32[4096]{0:T(1024)S(1)} fusion(s32[349696]{0:T(1024)S(1)} %get-tuple-element.426, s32[4096]{0:T(1024)S(1)} %fusion.66), kind=kCustom, calls=%fused_computation.1.clone.1 | custom fusion | bytes 49152 | tf_op jit(solution)/shard_map/while/body/gather | solution.py:106
  290.5 25.9 %gather_fusion = s32[4096]{0:T(1024)S(1)} fusion(s32[512]{0:T(512)S(1)} %get-tuple-element.424, s32[4096]{0:T(1024)S(1)} %fusion.64), kind=kCustom, calls=%fused_computation.clone.1 | custom fusion | bytes 49152 | tf_op jit(solution)/shard_map/while/body/gather | solution.py:38
  316.4 24.7 %gather_fusion.4 = s32[4096]{0:T(1024)S(1)} fusion(s32[128]{0:T(128)S(1)} %get-tuple-element.428, s32[4096]{0:T(1024)S(1)} %get-tuple-element.384), kind=kCustom, calls=%fused_computation.2.clone.1 | custom fusion | bytes 49152 | tf_op jit(solution)/shard_map/while/body/gather | solution.py:38
  341.1 0.1 fusion.67
  341.2 23.0 %gather_fusion.3 = s32[4096]{0:T(1024)S(1)} fusion(s32[2048]{0:T(1024)S(1)} %get-tuple-element.430, s32[4096]{0:T(1024)S(1)} %get-tuple-element.383), kind=kCustom, calls=%fused_computation.3.clone.1 | custom fusion | bytes 49152 | tf_op jit(solution)/shard_map/while/body/gather | solution.py:38
  364.2 1.4 fusion.68
  365.6 0.7 fusion.69
  366.3 0.6 reshape.44
  366.9 480.6 %all-reduce.2.cloned.1.call-done = f32[16,1024]{1,0:T(8,128)} async-done(((f32[16,1024]{1,0:T(8,128)}), f32[16,1024]{1,0:T(8,128)}) %all-reduce.2.cloned.1.call-update) | async-done | bytes 65552 | tf_op jit(solution)/shard_map/psum | solution.py:125
  847.5 1.5 copy.22
  (16 shorter events, 0.3 us)
Async XLA Ops:
  174.5 57.2 %all-to-all-start = ((s32[4,1,87424]{2,1,0:T(1,128)}), s32[4,1,87424]{2,1,0:T(1,128)S(1)}, u32[]{:S(2)}, u32[]{:S(2)}) async-start(s32[4,1,87424]{2,1,0:T(1,128)} %broadcast_in_dim.75), calls=%async_computation | async-start | bytes 2797568 | tf_op jit(solution)/shard_map/all_to_all | solution.py:28
  232.4 11.7 %all-to-all-start.1 = ((s32[4,1,8192]{2,1,0:T(1,128)}), s32[4,1,8192]{2,1,0:T(1,128)S(1)}, u32[]{:S(2)}, u32[]{:S(2)}) async-start(s32[4,1,8192]{2,1,0:T(1,128)} %broadcast_in_dim.77), calls=%async_computation.1 | async-start | bytes 262144 | tf_op jit(solution)/shard_map/all_to_all | solution.py:28
  236.6 610.9 %all-reduce.2.cloned.1.call-start = ((), (), s32[]{:S(2)}) async-start(), calls=%async_computation.2 | async-start | bytes 131072 | tf_op jit(solution)/shard_map/psum | solution.py:125
  242.1 2.0 copy-start
  242.1 2.0 copy-start.1
  242.1 2.0 copy-start.2
Sparse Core Ops, SparseCore 0:
  367.0 480.4 all-reduce.1
where the time goes:
time: 856 us
  waiting for transfers between devices  503 us (59%)
  blocking collectives  163 us (19%)
  local copies, waits for them, and re-layouts  128 us (15%)
  starting transfers between devices  40.3 us (5%)
  between operations  14.2 us (2%)
    psum x1, waiting for transfers between devices, shards(): result = lax.psum(group_sums, ('gx', 'gy'))  481 us
    all_gather x1, blocking collectives, gather_together(): lines, at, outs = (lax.all_gather(flat, axis), 0, [])  163 us
    gather x3, local copies, waits for them, and re-layouts, pick_bits(): chosen = packed[position // per_word]  73.6 us
    all_to_all x2, starting transfers between devices, from_everyone(): return lax.all_to_all(copies, axis, split_axis=0, concat_axis=0, tiled=True)  40.3 us
    gather x1, local copies, waits for them, and re-layouts, add_block(): flag_word = product_bits[flag_place(owner_idx, local_idx // 32)]  23 us
    gather x1, local copies, waits for them, and re-layouts, add_block(): word_val = brand_table[brand_place(owner_idx, local_idx // 3)]  23 us
    all_to_all x2, waiting for transfers between devices, from_everyone(): return lax.all_to_all(copies, axis, split_axis=0, concat_axis=0, tiled=True)  22.5 us
  transfers between devices with their start and end apart: 3, of which 3 were waited for; matrix products, arithmetic and copies ran while one was open for 1% of the time, Pallas kernels for 0%

commit v1 on v0

--- a/solution.py
+++ b/solution.py
@@ -122,7 +122,7 @@
 
     totals = lax.fori_loop(0, block_total, add_block, jnp.zeros((high_groups, 128), jnp.float32))
     group_sums = totals.reshape(YEARS, BRANDS)
-    result = lax.psum(group_sums, ("gx", "gy"))
+    result = jnp.sum(lax.all_gather(group_sums, ("gx", "gy")), axis=0)
     return result
 
 

time: 856 us -> 1050 us (1.23)
  waiting for transfers between devices: 503 us -> 690 us
    all_gather x0 -> x1, waiting for transfers between devices: none -> 667 us  [shards(): result = jnp.sum(lax.all_gather(group_sums, ('gx', 'gy')), axis=0)]
    psum x1 -> x0, waiting for transfers between devices: 481 us -> none  [shards(): result = lax.psum(group_sums, ('gx', 'gy'))]
where the time goes in v1:
time: 1050 us
  waiting for transfers between devices  690 us (66%)
  blocking collectives  163 us (16%)
  local copies, waits for them, and re-layouts  127 us (12%)
  starting transfers between devices  40.3 us (4%)
  between operations  14.2 us (1%)
  other arithmetic  13.2 us (1%)
    all_gather x1, waiting for transfers between devices, shards(): result = jnp.sum(lax.all_gather(group_sums, ('gx', 'gy')), axis=0)  667 us
    all_gather x1, blocking collectives, gather_together(): lines, at, outs = (lax.all_gather(flat, axis), 0, [])  163 us
    gather x3, local copies, waits for them, and re-layouts, pick_bits(): chosen = packed[position // per_word]  73.6 us
    all_to_all x2, starting transfers between devices, from_everyone(): return lax.all_to_all(copies, axis, split_axis=0, concat_axis=0, tiled=True)  40.3 us
    gather x1, local copies, waits for them, and re-layouts, add_block(): flag_word = product_bits[flag_place(owner_idx, local_idx // 32)]  23 us
    gather x1, local copies, waits for them, and re-layouts, add_block(): word_val = brand_table[brand_place(owner_idx, local_idx // 3)]  23 us
    all_to_all x2, waiting for transfers between devices, from_everyone(): return lax.all_to_all(copies, axis, split_axis=0, concat_axis=0, tiled=True)  22.5 us
  transfers between devices with their start and end apart: 3, of which 3 were waited for; matrix products, arithmetic and copies ran while one was open for 1% of the time, Pallas kernels for 0%

profile of v1, /device:TPU:1, one launch (start us, length us, event | category | flops | bytes accessed | tf_op | source)
XLA Modules:
  0.0 1048.5 jit_solution(2414784116842742830)
XLA Ops:
  6.5 0.8 dynamic_slice.34
  7.3 0.8 dynamic_slice.35
  8.1 0.8 concatenate.3
  8.8 163.3 %all-gather.1 = s32[64,1,1536]{2,1,0:T(1,128)S(1)} all-gather(s32[1,1,1536]{2,1,0:T(1,128)S(1)} %reshape.87), channel_id=2, replica_groups=mesh['gx'=64,'gy'=4] {'gx'}, dimensions={0}, use_global_device_ids=true | all-gather | bytes 399360 | tf_op jit(solution)/shard_map/all_gather | solution.py:18
  172.2 0.1 slice.31
  172.4 0.3 broadcast_in_dim.74
  172.7 1.8 broadcast_in_dim.75
  174.5 36.1 %all-to-all-start = ((s32[4,1,87424]{2,1,0:T(1,128)}), s32[4,1,87424]{2,1,0:T(1,128)S(1)}, u32[]{:S(2)}, u32[]{:S(2)}) async-start(s32[4,1,87424]{2,1,0:T(1,128)} %broadcast_in_dim.75), calls=%async_computation | async-start | bytes 2797568 | tf_op jit(solution)/shard_map/all_to_all | solution.py:28
  210.5 0.1 slice_bitcast_fusion
  210.6 21.0 %all-to-all-done = s32[4,1,87424]{2,1,0:T(1,128)S(1)} async-done(((s32[4,1,87424]{2,1,0:T(1,128)}), s32[4,1,87424]{2,1,0:T(1,128)S(1)}, u32[]{:S(2)}, u32[]{:S(2)}) %all-to-all-start) | async-done | bytes 1398816 | tf_op jit(solution)/shard_map/all_to_all | solution.py:28
  231.7 0.7 broadcast_in_dim.77
  232.4 4.3 all-to-all-start.1
  237.3 0.1 slice.33
  237.4 0.1 slice.32
  237.5 0.1 reshape.39
  237.6 0.1 reshape.38
  237.7 0.1 reshape.36
  237.8 4.3 reduce
  242.1 0.6 reshape.37
  242.7 1.4 all-to-all-done.1
  244.2 122.1 %while.13 = (s32[]{:T(128)}, f32[128,128]{1,0:T(8,128)S(1)}, s32[]{:T(128)}, s32[12288]{0:T(1024)S(1)}, s32[512]{0:T(512)S(1)}, /*index=5*/s32[12288]{0:T(1024)S...) while((s32[]{:T(128)}, f32[128,128]{1,0:T(8,128)S(1)}, ...), condition=%wide.region_1.2_spmd, body=%wide.region_0.1_spmd.sunk | while | flops 136892416 | bytes 860395 | solution.py:123
  244.2 23.0 %gather_fusion.2 = s32[4096]{0:T(1024)S(1)} fusion(s32[32768]{0:T(1024)S(1)} %get-tuple-element.431, s32[4096]{0:T(1024)S(1)} %get-tuple-element.382), kind=kCustom, calls=%fused_computation.4.clone.1 | custom fusion | bytes 49152 | tf_op jit(solution)/shard_map/while/body/gather | solution.py:99
  267.4 23.0 %gather_fusion.1 = s32[4096]{0:T(1024)S(1)} fusion(s32[349696]{0:T(1024)S(1)} %get-tuple-element.426, s32[4096]{0:T(1024)S(1)} %fusion.66), kind=kCustom, calls=%fused_computation.1.clone.1 | custom fusion | bytes 49152 | tf_op jit(solution)/shard_map/while/body/gather | solution.py:106
  290.5 25.9 %gather_fusion = s32[4096]{0:T(1024)S(1)} fusion(s32[512]{0:T(512)S(1)} %get-tuple-element.424, s32[4096]{0:T(1024)S(1)} %fusion.64), kind=kCustom, calls=%fused_computation.clone.1 | custom fusion | bytes 49152 | tf_op jit(solution)/shard_map/while/body/gather | solution.py:38
  316.4 24.7 %gather_fusion.4 = s32[4096]{0:T(1024)S(1)} fusion(s32[128]{0:T(128)S(1)} %get-tuple-element.428, s32[4096]{0:T(1024)S(1)} %get-tuple-element.384), kind=kCustom, calls=%fused_computation.2.clone.1 | custom fusion | bytes 49152 | tf_op jit(solution)/shard_map/while/body/gather | solution.py:38
  341.1 0.1 fusion.67
  341.2 23.0 %gather_fusion.3 = s32[4096]{0:T(1024)S(1)} fusion(s32[2048]{0:T(1024)S(1)} %get-tuple-element.430, s32[4096]{0:T(1024)S(1)} %get-tuple-element.383), kind=kCustom, calls=%fused_computation.3.clone.1 | custom fusion | bytes 49152 | tf_op jit(solution)/shard_map/while/body/gather | solution.py:38
  364.2 1.4 fusion.68
  365.6 0.7 fusion.69
  366.3 0.6 all_gather_reshape.3
  366.9 667.5 %all-gather.4.cloned.1.call-done = f32[256,16,1024]{2,1,0:T(8,128)} async-done(((f32[1,16,1024]{2,1,0:T(8,128)}), f32[256,16,1024]{2,1,0:T(8,128)}) %all-gather.4.cloned.1.call-update) | async-done | bytes 16777232 | tf_op jit(solution)/shard_map/all_gather | solution.py:125
  1034.4 7.3 reduce_sum.9
  (16 shorter events, 0.3 us)
Async XLA Ops:
  174.5 57.2 %all-to-all-start = ((s32[4,1,87424]{2,1,0:T(1,128)}), s32[4,1,87424]{2,1,0:T(1,128)S(1)}, u32[]{:S(2)}, u32[]{:S(2)}) async-start(s32[4,1,87424]{2,1,0:T(1,128)} %broadcast_in_dim.75), calls=%async_computation | async-start | bytes 2797568 | tf_op jit(solution)/shard_map/all_to_all | solution.py:28
  232.4 11.7 %all-to-all-start.1 = ((s32[4,1,8192]{2,1,0:T(1,128)}), s32[4,1,8192]{2,1,0:T(1,128)S(1)}, u32[]{:S(2)}, u32[]{:S(2)}) async-start(s32[4,1,8192]{2,1,0:T(1,128)} %broadcast_in_dim.77), calls=%async_computation.1 | async-start | bytes 262144 | tf_op jit(solution)/shard_map/all_to_all | solution.py:28
  236.6 797.7 %all-gather.4.cloned.1.call-start = ((), (), s32[]{:S(2)}) async-start(), calls=%async_computation.2 | async-start | bytes 16842752 | tf_op jit(solution)/shard_map/all_gather | solution.py:125
  242.1 2.0 copy-start
  242.1 2.0 copy-start.1
  242.1 2.0 copy-start.2
Sparse Core Ops, SparseCore 0:
  367.0 667.2 all-gather.3

commit v2 on v0

--- a/solution.py
+++ b/solution.py
@@ -122,7 +122,7 @@
 
     totals = lax.fori_loop(0, block_total, add_block, jnp.zeros((high_groups, 128), jnp.float32))
     group_sums = totals.reshape(YEARS, BRANDS)
-    result = lax.psum(group_sums, ("gx", "gy"))
+    result = lax.psum(lax.psum(group_sums, "gy"), "gx")
     return result
 
 

time: 856 us -> 1290 us (1.51); the launches traced: 856 us -> 1270 us
  waiting for transfers between devices: 503 us -> 921 us
    psum x1 -> x2, waiting for transfers between devices: 481 us -> 898 us  [shards(): result = lax.psum(lax.psum(group_sums, 'gy'), 'gx')]
  transfers between devices with their start and end apart: 3 -> 4, of which waited for: 3 -> 4; matrix products, arithmetic and copies ran while one was open for 1% -> 0% of each run, Pallas kernels for 0% -> 0%
where the time goes in v2:
time: 1290 us; the launch traced here: 1270 us
  waiting for transfers between devices  921 us (71%)
  blocking collectives  163 us (13%)
  local copies, waits for them, and re-layouts  128 us (10%)
  starting transfers between devices  40.4 us (3%)
  between operations  14.2 us (1%)
    psum x2, waiting for transfers between devices, shards(): result = lax.psum(lax.psum(group_sums, 'gy'), 'gx')  898 us
    all_gather x1, blocking collectives, gather_together(): lines, at, outs = (lax.all_gather(flat, axis), 0, [])  163 us
    gather x3, local copies, waits for them, and re-layouts, pick_bits(): chosen = packed[position // per_word]  73.6 us
    all_to_all x2, starting transfers between devices, from_everyone(): return lax.all_to_all(copies, axis, split_axis=0, concat_axis=0, tiled=True)  40.3 us
  transfers between devices with their start and end apart: 4, of which 4 were waited for; matrix products, arithmetic and copies ran while one was open for 0% of the time, Pallas kernels for 0%

profile of v2, /device:TPU:1, one launch (start us, length us, event | category | flops | bytes accessed | tf_op | source)
XLA Modules:
  0.0 1273.8 jit_solution(14581728172765101583)
XLA Ops:
  6.5 0.8 dynamic_slice.34
  7.3 0.8 dynamic_slice.35
  8.1 0.8 concatenate.3
  8.8 163.3 %all-gather.1 = s32[64,1,1536]{2,1,0:T(1,128)S(1)} all-gather(s32[1,1,1536]{2,1,0:T(1,128)S(1)} %reshape.91), channel_id=2, replica_groups=mesh['gx'=64,'gy'=4] {'gx'}, dimensions={0}, use_global_device_ids=true | all-gather | bytes 399360 | tf_op jit(solution)/shard_map/all_gather | solution.py:18
  172.2 0.1 slice.31
  172.4 0.3 broadcast_in_dim.74
  172.7 1.8 broadcast_in_dim.75
  174.5 36.1 %all-to-all-start = ((s32[4,1,87424]{2,1,0:T(1,128)}), s32[4,1,87424]{2,1,0:T(1,128)S(1)}, u32[]{:S(2)}, u32[]{:S(2)}) async-start(s32[4,1,87424]{2,1,0:T(1,128)} %broadcast_in_dim.75), calls=%async_computation | async-start | bytes 2797568 | tf_op jit(solution)/shard_map/all_to_all | solution.py:28
  210.5 0.1 slice_bitcast_fusion
  210.6 21.0 %all-to-all-done = s32[4,1,87424]{2,1,0:T(1,128)S(1)} async-done(((s32[4,1,87424]{2,1,0:T(1,128)}), s32[4,1,87424]{2,1,0:T(1,128)S(1)}, u32[]{:S(2)}, u32[]{:S(2)}) %all-to-all-start) | async-done | bytes 1398816 | tf_op jit(solution)/shard_map/all_to_all | solution.py:28
  231.7 0.7 broadcast_in_dim.77
  232.4 4.3 all-to-all-start.1
  237.3 0.1 slice.33
  237.4 0.1 slice.32
  237.6 0.1 reshape.41
  237.7 0.1 reshape.39
  237.8 4.3 reduce
  242.1 0.6 reshape.40
  242.7 1.4 all-to-all-done.1
  244.2 122.1 %while.13 = (s32[]{:T(128)}, f32[128,128]{1,0:T(8,128)S(1)}, s32[]{:T(128)}, s32[12288]{0:T(1024)S(1)}, s32[512]{0:T(512)S(1)}, /*index=5*/s32[12288]{0:T(1024)S...) while((s32[]{:T(128)}, f32[128,128]{1,0:T(8,128)S(1)}, ...), condition=%wide.region_1.2_spmd, body=%wide.region_0.1_spmd.sunk | while | flops 136892416 | bytes 860395 | solution.py:123
  244.2 23.0 %gather_fusion.2 = s32[4096]{0:T(1024)S(1)} fusion(s32[32768]{0:T(1024)S(1)} %get-tuple-element.431, s32[4096]{0:T(1024)S(1)} %get-tuple-element.382), kind=kCustom, calls=%fused_computation.4.clone.1 | custom fusion | bytes 49152 | tf_op jit(solution)/shard_map/while/body/gather | solution.py:99
  267.4 23.0 %gather_fusion.1 = s32[4096]{0:T(1024)S(1)} fusion(s32[349696]{0:T(1024)S(1)} %get-tuple-element.426, s32[4096]{0:T(1024)S(1)} %fusion.66), kind=kCustom, calls=%fused_computation.1.clone.1 | custom fusion | bytes 49152 | tf_op jit(solution)/shard_map/while/body/gather | solution.py:106
  290.5 25.9 %gather_fusion = s32[4096]{0:T(1024)S(1)} fusion(s32[512]{0:T(512)S(1)} %get-tuple-element.424, s32[4096]{0:T(1024)S(1)} %fusion.64), kind=kCustom, calls=%fused_computation.clone.1 | custom fusion | bytes 49152 | tf_op jit(solution)/shard_map/while/body/gather | solution.py:38
  316.4 24.7 %gather_fusion.4 = s32[4096]{0:T(1024)S(1)} fusion(s32[128]{0:T(128)S(1)} %get-tuple-element.428, s32[4096]{0:T(1024)S(1)} %get-tuple-element.384), kind=kCustom, calls=%fused_computation.2.clone.1 | custom fusion | bytes 49152 | tf_op jit(solution)/shard_map/while/body/gather | solution.py:38
  341.1 0.1 fusion.67
  341.2 23.0 %gather_fusion.3 = s32[4096]{0:T(1024)S(1)} fusion(s32[2048]{0:T(1024)S(1)} %get-tuple-element.430, s32[4096]{0:T(1024)S(1)} %get-tuple-element.383), kind=kCustom, calls=%fused_computation.3.clone.1 | custom fusion | bytes 49152 | tf_op jit(solution)/shard_map/while/body/gather | solution.py:38
  364.2 1.4 fusion.68
  365.6 0.7 fusion.69
  366.3 0.6 reshape.44
  367.0 291.6 %all-reduce.3.cloned.1.call-done = f32[16,1024]{1,0:T(8,128)} async-done(((f32[16,1024]{1,0:T(8,128)}), f32[16,1024]{1,0:T(8,128)}) %all-reduce.3.cloned.1.call-update) | async-done | bytes 65552 | tf_op jit(solution)/shard_map/psum | solution.py:125
  658.7 606.8 %all-reduce.5.cloned.1.call-done = f32[16,1024]{1,0:T(8,128)} async-done(((f32[16,1024]{1,0:T(8,128)}), f32[16,1024]{1,0:T(8,128)}) %all-reduce.5.cloned.1.call-update) | async-done | bytes 65552 | tf_op jit(solution)/shard_map/psum | solution.py:125
  1265.5 1.5 copy.23
  (19 shorter events, 0.4 us)
Async XLA Ops:
  174.5 57.2 %all-to-all-start = ((s32[4,1,87424]{2,1,0:T(1,128)}), s32[4,1,87424]{2,1,0:T(1,128)S(1)}, u32[]{:S(2)}, u32[]{:S(2)}) async-start(s32[4,1,87424]{2,1,0:T(1,128)} %broadcast_in_dim.75), calls=%async_computation | async-start | bytes 2797568 | tf_op jit(solution)/shard_map/all_to_all | solution.py:28
  232.4 11.7 all-to-all-start.1
  236.6 422.0 %all-reduce.3.cloned.1.call-start = ((), (), s32[]{:S(2)}) async-start(), calls=%async_computation.2 | async-start | bytes 131072 | tf_op jit(solution)/shard_map/psum | solution.py:125
  242.1 2.0 copy-start
  242.1 2.0 copy-start.1
  242.1 2.0 copy-start.2
  366.9 898.6 %all-reduce.5.cloned.1.call-start = ((), (), s32[]{:S(2)}) async-start(), calls=%async_computation.3 | async-start | bytes 131072 | tf_op jit(solution)/shard_map/psum | solution.py:125
Sparse Core Ops, SparseCore 0:
  367.0 291.5 all-reduce.2
  661.2 604.2 all-reduce.4
